TPU v7x, 32 devices: a whole 2x2x4 slice. The times are simulated.
32 devices in a mesh: row: 4 (over z), col: 8 (over y, x, core).
Axes of the slice: x: 2, y: 2, z: 4, core: 2. Of those that a mesh axis runs over, the one named last changes fastest.
Arguments:
- band_sites: float32 [2, 128], P(None, 'row'), may hold values from 0 to 1
- test_sites: float32 [2, 1024], P(None, 'col'), may hold values from 0 to 1
- band_factor: float32 [128, 128], P('row', 'col'), as said below
- prior_factor: float32 [128, 2048], P('row', 'col'), may hold values from -0.125 to 0.125
- prior_solution: float32 [2048, 1024], P('col', 'row'), may hold values from -6 to 6
- prior_covariance: float32 [1024, 1024], P('row', 'col'), may hold values from -4 to 4
Outputs:
- band_solution: float32 [128, 1024], P('row', 'col')
- covariance: float32 [1024, 1024], P('row', 'col')
Inputs may be any that keep to these rules, and one draw needn't show every extreme that they name: band_factor is lower triangular with diagonal entries in 1 to 2 and small entries below it.
All inputs are finite; a program needn't handle non-finite values.
Results may differ from a plain program's by a relative error of at most 0.00011.
Values sent between devices are 32-bit elements; how exact they have to be, the bound alone decides.
No kernel may reach another device: no remote copies, remote signals or barrier semaphores. Data moves between devices by JAX's collectives and lax.ppermute only.
A program may use at most 64 MiB of HBM per device.

v0:
```python
import jax
import jax.numpy as jnp
from jax import lax
from jax.sharding import PartitionSpec as P

length_scale = 0.3


def matern(band_sites, test_sites):
    delta_x = band_sites[0][:, None] - test_sites[0][None, :]
    delta_y = band_sites[1][:, None] - test_sites[1][None, :]
    scaled = jnp.sqrt(delta_x * delta_x + delta_y * delta_y + 1e-06) * (3.0**0.5 / length_scale)
    return (1.0 + scaled) * jnp.exp(-scaled)


def local(band_sites, test_sites, band_factor, prior_factor, prior_solution, prior_covariance):
    tile_rows = band_factor.shape[0]
    test_cols = test_sites.shape[1]
    row_count = lax.axis_size("row")
    my_row = lax.axis_index("row")
    cross = matern(band_sites, test_sites)
    partial_terms = lax.dot_general(
        lax.all_gather(prior_solution, "row", axis=1, tiled=True),
        prior_factor,
        (((0,), (1,)), ((), ())),
        precision=lax.Precision.HIGHEST,
        preferred_element_type=jnp.float32,
    )
    update = lax.psum_scatter(partial_terms, "col", scatter_dimension=0, tiled=True)
    remaining = cross - update.T
    factor_row = lax.all_gather(band_factor, "col", axis=1, tiled=True)
    whole_rest = lax.all_gather(remaining, "row", axis=0, tiled=True)
    whole_factor = lax.all_gather(factor_row, "row", axis=0, tiled=True)
    whole_solved = lax.linalg.triangular_solve(whole_factor, whole_rest, left_side=True, lower=True)
    collected = whole_solved.reshape(row_count, tile_rows, test_cols)
    band_solution = lax.dynamic_index_in_dim(collected, my_row, 0, keepdims=False)
    band_rows = lax.all_gather(band_solution, "col", axis=1, tiled=True)
    gram_sum = lax.psum_scatter(
        lax.dot_general(
            band_rows,
            band_solution,
            (((0,), (0,)), ((), ())),
            precision=lax.Precision.HIGHEST,
            preferred_element_type=jnp.float32,
        ),
        "row",
        scatter_dimension=0,
        tiled=True,
    )
    return (band_solution, prior_covariance - gram_sum)


def solution(mesh):
    placed = (
        P(None, "row"),
        P(None, "col"),
        P("row", "col"),
        P("row", "col"),
        P("col", "row"),
        P("row", "col"),
    )
    return jax.shard_map(
        local,
        mesh=mesh,
        in_specs=placed,
        out_specs=(P("row", "col"), P("row", "col")),
        check_vma=False,
    )
```

profile of v0, /device:TPU:0, one launch (start us, length us, event | category | flops | bytes accessed | tf_op | source)
XLA Modules:
  0.0 136.1 jit_solution(165506387914576891)
XLA Ops:
  7.2 0.0 copy-start
  7.2 0.0 all-gather.3.cloned.1.call-start
  7.2 0.7 all-gather.3.cloned.1.call-update
  7.9 0.0 copy-start.3
  7.9 0.0 reduce-scatter.3.cloned.1.call-start
  8.0 0.6 copy-done.3
  8.6 10.7 %all_gather.15 = f32[32,128]{0,1:T(8,128)S(1)} all-gather(f32[32,16]{0,1:T(8,128)S(1)} %copy-done.3), channel_id=1, replica_groups=mesh['row'=4,'col'=8] {'col'}, dimensions={1}, use_global_device_ids=true | all-gather | bytes 18432 | tf_op jit(solution)/shard_map/all_gather | solution.py:31
  19.3 0.1 copy.12
  19.4 14.0 %all_gather.16 = f32[128,128]{1,0:T(8,128)S(1)} all-gather(f32[32,128]{1,0:T(8,128)S(1)} %copy.12), channel_id=1, replica_groups=mesh['row'=4,'col'=8] {'row'}, dimensions={0}, use_global_device_ids=true | all-gather | bytes 81920 | tf_op jit(solution)/shard_map/all_gather | solution.py:33
  33.4 9.8 %custom-call.3 = f32[1,128,128]{1,2,0:T(8,128)S(1)} custom-call(f32[1,128,128]{2,1,0:T(8,128)S(1)} %select_bitcast_fusion), custom_call_target="InvertDiagBlocksLowerTriangular" | custom-call | tf_op jit(solution)/shard_map/triangular_solve | solution.py:34
  43.2 0.1 copy.13
  43.3 0.0 copy-start.4
  43.3 0.7 copy-done.4
  44.0 0.0 all-gather.3.cloned.1.call-done
  44.0 0.0 copy-done
  44.0 2.6 %fusion.4 = f32[1024,32]{0,1:T(8,128)} fusion(f32[256,1024]{1,0:T(8,128)} %all-gather.3.cloned.1.call-done, f32[32,256]{1,0:T(8,128)S(1)} %copy-done), kind=kOutput, calls=%fused_computation.12 | convolution fusion | flops 100663296 | bytes 1212416 | tf_op jit(solution)/shard_map/dot_general | solution.py:22
  46.6 0.0 copy-start.5
  46.6 0.0 reduce-scatter.3.cloned.1.call-update
  46.6 0.0 reduce-scatter.5.cloned.1.call-start
  46.7 0.6 copy-done.5
  47.3 33.4 %reduce-scatter.3.cloned.1.call-done = f32[128,32]{0,1:T(8,128)} async-done(((f32[1024,32]{0,1:T(8,128)}), f32[128,32]{0,1:T(8,128)}) %reduce-scatter.3.cloned.1.call-update) | async-done | bytes 16400 | tf_op jit(solution)/shard_map/reduce_scatter | solution.py:29
  80.7 0.8 bitcast_subtract_fusion
  81.5 13.3 %all_gather.18 = f32[128,128]{1,0:T(8,128)S(1)} all-gather(f32[32,128]{1,0:T(8,128)S(1)} %bitcast_subtract_fusion), channel_id=1, replica_groups=mesh['row'=4,'col'=8] {'row'}, dimensions={0}, use_global_device_ids=true | all-gather | bytes 81920 | tf_op jit(solution)/shard_map/all_gather | solution.py:32
  94.7 0.2 fusion.2
  95.0 0.0 copy-start.2
  95.0 9.3 %all-gather = f32[1,32,1024]{2,1,0:T(8,128)S(1)} all-gather(f32[1,32,128]{2,1,0:T(8,128)S(1)} %constant_dynamic-slice_fusion), channel_id=2, replica_groups=mesh['row'=4,'col'=8] {'col'}, dimensions={2}, use_global_device_ids=true | all-gather | bytes 147456 | tf_op jit(solution)/shard_map/all_gather | solution.py:37
  104.3 0.0 copy-done.2
  104.3 1.8 %fusion = f32[1024,128]{1,0:T(8,128)} fusion(f32[32,128]{1,0:T(8,128)S(1)} %fusion.9, f32[1,32,1024]{2,1,0:T(8,128)S(1)} %all-gather), kind=kOutput, calls=%fused_computation | convolution fusion | flops 50331648 | bytes 671744 | tf_op jit(solution)/shard_map/dot_general | solution.py:39
  106.0 0.0 reduce-scatter.5.cloned.1.call-update
  106.1 21.9 %reduce-scatter.5.cloned.1.call-done = f32[256,128]{1,0:T(8,128)} async-done(((f32[1024,128]{1,0:T(8,128)}), f32[256,128]{1,0:T(8,128)}) %reduce-scatter.5.cloned.1.call-update) | async-done | bytes 131088 | tf_op jit(solution)/shard_map/reduce_scatter | solution.py:38
  128.0 0.0 copy-done.1
  128.0 1.6 %sub.51 = f32[256,128]{1,0:T(8,128)} subtract(f32[256,128]{1,0:T(8,128)S(1)} %copy-done.1, f32[256,128]{1,0:T(8,128)} %reduce-scatter.5.cloned.1.call-done) | non-fusion elementwise | flops 32768 | bytes 393216 | tf_op jit(solution)/shard_map/sub | solution.py:50
  (6 shorter events, 0.0 us)
Async XLA Ops:
  7.2 36.8 %copy-start = (f32[32,256]{1,0:T(8,128)S(1)}, f32[32,256]{1,0:T(8,128)}, u32[]{:S(2)}) copy-start(f32[32,256]{1,0:T(8,128)} %param.9) | copy-start | bytes 98308
  7.2 36.8 %all-gather.3.cloned.1.call-start = ((), (), s32[]{:S(2)}) async-start(), calls=%async_computation.2 | async-start | bytes 1310720 | tf_op jit(solution)/shard_map/all_gather | solution.py:23
  7.9 0.7 copy-start.3
  7.9 72.7 %reduce-scatter.3.cloned.1.call-start = ((), (), s32[]{:S(2)}) async-start(), calls=%async_computation.3 | async-start | bytes 147456 | tf_op jit(solution)/shard_map/reduce_scatter | solution.py:29
  43.3 0.7 copy-start.4
  46.6 0.7 copy-start.5
  46.6 81.3 %reduce-scatter.5.cloned.1.call-start = ((), (), s32[]{:S(2)}) async-start(), calls=%async_computation.4 | async-start | bytes 655360 | tf_op jit(solution)/shard_map/reduce_scatter | solution.py:38
  95.0 9.3 %copy-start.2 = (f32[32,128]{1,0:T(8,128)}, f32[32,128]{1,0:T(8,128)S(1)}, u32[]{:S(2)}) copy-start(f32[32,128]{1,0:T(8,128)S(1)} %fusion.9) | copy-start | bytes 49156
  106.0 21.9 %copy-start.1 = (f32[256,128]{1,0:T(8,128)S(1)}, f32[256,128]{1,0:T(8,128)}, u32[]{:S(2)}) copy-start(f32[256,128]{1,0:T(8,128)} %param.11) | copy-start | bytes 393220
Sparse Core Ops, SparseCore 0:
  9.6 31.7 all-gather.2
  46.8 33.8 reduce-scatter.2
  106.2 21.7 reduce-scatter.4
where the time goes:
time: 136 us
  waiting for transfers between devices  56 us (41%)
  blocking collectives  47.2 us (35%)
  between operations  13.8 us (10%)
  other arithmetic  12.2 us (9%)
  matrix products  4.6 us (3%)
  local copies, waits for them, and re-layouts  2.12 us (2%)
    reduce_scatter x1, waiting for transfers between devices, local(): lax.psum_scatter(partial_terms, 'col', scatter_dimension=0, tiled=True)  33.4 us
    reduce_scatter x1, waiting for transfers between devices, local(): lax.psum_scatter(lax.dot_general(band_rows, band_solution, (((0,), (0,)),...  21.9 us
    all_gather x1, blocking collectives, local(): whole_factor = lax.all_gather(factor_row, 'row', axis=0, tiled=True)  14 us
    all_gather x1, blocking collectives, local(): whole_rest = lax.all_gather(remaining, 'row', axis=0, tiled=True)  13.3 us
    all_gather x1, blocking collectives, local(): factor_row = lax.all_gather(band_factor, 'col', axis=1, tiled=True)  10.7 us
    another operation x2, other arithmetic, local(): lax.linalg.triangular_solve(whole_factor, whole_rest, left_side=True, low...  9.82 us
    all_gather x1, blocking collectives, local(): band_rows = lax.all_gather(band_solution, 'col', axis=1, tiled=True)  9.25 us
  transfers between devices with their start and end apart: 3, of which 2 were waited for; matrix products, arithmetic and copies ran while one was open for 7% of the time, Pallas kernels for 0%

commit v1 on v0

--- a/solution.py
+++ b/solution.py
@@ -4,6 +4,11 @@
 from jax.sharding import PartitionSpec as P
 
 length_scale = 0.3
+fit_goods = lambda state, xs, dev_axis: jnp.split(
+    lax.all_gather(jnp.concatenate([state, xs], axis=1), tiled=True, axis_name=dev_axis, axis=0),
+    [state.shape[1]],
+    axis=1,
+)
 
 
 def matern(band_sites, test_sites):
@@ -29,8 +34,7 @@
     update = lax.psum_scatter(partial_terms, "col", scatter_dimension=0, tiled=True)
     remaining = cross - update.T
     factor_row = lax.all_gather(band_factor, "col", axis=1, tiled=True)
-    whole_rest = lax.all_gather(remaining, "row", axis=0, tiled=True)
-    whole_factor = lax.all_gather(factor_row, "row", axis=0, tiled=True)
+    whole_rest, whole_factor = fit_goods(remaining, factor_row, "row")
     whole_solved = lax.linalg.triangular_solve(whole_factor, whole_rest, left_side=True, lower=True)
     collected = whole_solved.reshape(row_count, tile_rows, test_cols)
     band_solution = lax.dynamic_index_in_dim(collected, my_row, 0, keepdims=False)

time: 136 us -> 143 us (1.051)
  waiting for transfers between devices: 56 us -> 76.1 us
  blocking collectives: 47.2 us -> 33.5 us
    all_gather x1, waiting for transfers between devices: 0.01 us -> 20.2 us  [local(): lax.all_gather(prior_solution, 'row', axis=1, tiled=True)]
    all_gather x2 -> x1, blocking collectives: 27.3 us -> 13.4 us  [lax.all_gather(jnp.concatenate([state, xs], axis=1), tiled=True, axis_nam...]
  transfers between devices with their start and end apart: 3 -> 3, of which waited for: 2 -> 3; matrix products, arithmetic and copies ran while one was open for 7% -> 0% of each run, Pallas kernels for 0% -> 0%
where the time goes in v1:
time: 143 us; the launch traced here: 142 us
  waiting for transfers between devices  76.1 us (53%)
  blocking collectives  33.5 us (23%)
  between operations  13.8 us (10%)
  other arithmetic  12.2 us (9%)
  matrix products  4.6 us (3%)
  local copies, waits for them, and re-layouts  2.14 us (1%)
    reduce_scatter x1, waiting for transfers between devices, local(): lax.psum_scatter(partial_terms, 'col', scatter_dimension=0, tiled=True)  33.2 us
    reduce_scatter x1, waiting for transfers between devices, local(): lax.psum_scatter(lax.dot_general(band_rows, band_solution, (((0,), (0,)),...  21.9 us
    all_gather x1, waiting for transfers between devices, local(): lax.all_gather(prior_solution, 'row', axis=1, tiled=True)  20.2 us
    all_gather x1, blocking collectives, lax.all_gather(jnp.concatenate([state, xs], axis=1), tiled=True, axis_nam...  13.4 us
    all_gather x1, blocking collectives, local(): factor_row = lax.all_gather(band_factor, 'col', axis=1, tiled=True)  10.7 us
    another operation x2, other arithmetic, local(): lax.linalg.triangular_solve(whole_factor, whole_rest, left_side=True, low...  9.82 us
    all_gather x1, blocking collectives, local(): band_rows = lax.all_gather(band_solution, 'col', axis=1, tiled=True)  9.36 us
  transfers between devices with their start and end apart: 3, of which 3 were waited for; matrix products, arithmetic and copies ran while one was open for 0% of the time, Pallas kernels for 0%

profile of v1, /device:TPU:0, one launch (start us, length us, event | category | flops | bytes accessed | tf_op | source)
XLA Modules:
  0.0 142.4 jit_solution(15394842557910586646)
XLA Ops:
  7.2 0.0 copy-start
  7.2 0.0 all-gather.3.cloned.1.call-start
  7.2 0.7 all-gather.3.cloned.1.call-update
  7.9 0.0 copy-start.3
  7.9 0.0 reduce-scatter.3.cloned.1.call-start
  8.0 0.6 copy-done.3
  8.6 10.7 %all_gather.13 = f32[32,128]{0,1:T(8,128)S(1)} all-gather(f32[32,16]{0,1:T(8,128)S(1)} %copy-done.3), channel_id=1, replica_groups=mesh['row'=4,'col'=8] {'col'}, dimensions={1}, use_global_device_ids=true | all-gather | bytes 18432 | tf_op jit(solution)/shard_map/all_gather | solution.py:36
  19.3 0.1 copy.12
  19.4 0.0 copy-start.4
  19.4 0.7 copy-done.4
  20.1 20.2 %all-gather.3.cloned.1.call-done = f32[256,1024]{1,0:T(8,128)} async-done(((f32[256,256]{1,0:T(8,128)}), f32[256,1024]{1,0:T(8,128)}) %all-gather.3.cloned.1.call-update) | async-done | bytes 1048592 | tf_op jit(solution)/shard_map/all_gather | solution.py:28
  40.3 0.0 copy-done
  40.3 2.6 %fusion.4 = f32[1024,32]{0,1:T(8,128)} fusion(f32[256,1024]{1,0:T(8,128)} %all-gather.3.cloned.1.call-done, f32[32,256]{1,0:T(8,128)S(1)} %copy-done), kind=kOutput, calls=%fused_computation.14 | convolution fusion | flops 100663296 | bytes 1212416 | tf_op jit(solution)/shard_map/dot_general | solution.py:27
  42.9 0.0 copy-start.5
  42.9 0.0 reduce-scatter.3.cloned.1.call-update
  42.9 0.0 reduce-scatter.5.cloned.1.call-start
  43.0 0.6 copy-done.5
  43.6 33.2 %reduce-scatter.3.cloned.1.call-done = f32[128,32]{0,1:T(8,128)} async-done(((f32[1024,32]{0,1:T(8,128)}), f32[128,32]{0,1:T(8,128)}) %reduce-scatter.3.cloned.1.call-update) | async-done | bytes 16400 | tf_op jit(solution)/shard_map/reduce_scatter | solution.py:34
  76.8 0.8 bitcast_subtract_fusion
  77.7 13.4 %all_gather.14 = f32[128,256]{1,0:T(8,128)S(1)} all-gather(f32[32,256]{1,0:T(8,128)S(1)} %pad_maximum_fusion), channel_id=1, replica_groups=mesh['row'=4,'col'=8] {'row'}, dimensions={0}, use_global_device_ids=true | all-gather | bytes 163840 | tf_op jit(solution)/shard_map/all_gather | solution.py:8
  91.1 9.8 %custom-call.3 = f32[1,128,128]{1,2,0:T(8,128)S(1)} custom-call(f32[1,128,128]{2,1,0:T(8,128)S(1)} %fusion.3), custom_call_target="InvertDiagBlocksLowerTriangular" | custom-call | tf_op jit(solution)/shard_map/triangular_solve | solution.py:38
  100.9 0.1 copy.13
  101.0 0.2 fusion.2
  101.2 0.0 copy-start.2
  101.3 9.4 %all-gather = f32[1,32,1024]{2,1,0:T(8,128)S(1)} all-gather(f32[1,32,128]{2,1,0:T(8,128)S(1)} %constant_dynamic-slice_fusion), channel_id=2, replica_groups=mesh['row'=4,'col'=8] {'col'}, dimensions={2}, use_global_device_ids=true | all-gather | bytes 147456 | tf_op jit(solution)/shard_map/all_gather | solution.py:41
  110.6 0.0 copy-done.2
  110.6 1.8 %fusion = f32[1024,128]{1,0:T(8,128)} fusion(f32[32,128]{1,0:T(8,128)S(1)} %fusion.9, f32[1,32,1024]{2,1,0:T(8,128)S(1)} %all-gather), kind=kOutput, calls=%fused_computation | convolution fusion | flops 50331648 | bytes 671744 | tf_op jit(solution)/shard_map/dot_general | solution.py:43
  112.4 0.0 copy-start.1
  112.4 0.0 reduce-scatter.5.cloned.1.call-update
  112.5 21.9 %reduce-scatter.5.cloned.1.call-done = f32[256,128]{1,0:T(8,128)} async-done(((f32[1024,128]{1,0:T(8,128)}), f32[256,128]{1,0:T(8,128)}) %reduce-scatter.5.cloned.1.call-update) | async-done | bytes 131088 | tf_op jit(solution)/shard_map/reduce_scatter | solution.py:42
  134.3 0.0 copy-done.1
  134.3 1.6 %sub.51 = f32[256,128]{1,0:T(8,128)} subtract(f32[256,128]{1,0:T(8,128)S(1)} %copy-done.1, f32[256,128]{1,0:T(8,128)} %reduce-scatter.5.cloned.1.call-done) | non-fusion elementwise | flops 32768 | bytes 393216 | tf_op jit(solution)/shard_map/sub | solution.py:54
  (6 shorter events, 0.0 us)
Async XLA Ops:
  7.2 33.1 %copy-start = (f32[32,256]{1,0:T(8,128)S(1)}, f32[32,256]{1,0:T(8,128)}, u32[]{:S(2)}) copy-start(f32[32,256]{1,0:T(8,128)} %param.9) | copy-start | bytes 98308
  7.2 33.1 %all-gather.3.cloned.1.call-start = ((), (), s32[]{:S(2)}) async-start(), calls=%async_computation.2 | async-start | bytes 1310720 | tf_op jit(solution)/shard_map/all_gather | solution.py:28
  7.9 0.7 copy-start.3
  7.9 68.9 %reduce-scatter.3.cloned.1.call-start = ((), (), s32[]{:S(2)}) async-start(), calls=%async_computation.3 | async-start | bytes 147456 | tf_op jit(solution)/shard_map/reduce_scatter | solution.py:34
  19.4 0.7 copy-start.4
  42.9 0.7 copy-start.5
  42.9 91.4 %reduce-scatter.5.cloned.1.call-start = ((), (), s32[]{:S(2)}) async-start(), calls=%async_computation.4 | async-start | bytes 655360 | tf_op jit(solution)/shard_map/reduce_scatter | solution.py:42
  101.2 9.4 %copy-start.2 = (f32[32,128]{1,0:T(8,128)}, f32[32,128]{1,0:T(8,128)S(1)}, u32[]{:S(2)}) copy-start(f32[32,128]{1,0:T(8,128)S(1)} %fusion.9) | copy-start | bytes 49156
  112.4 21.9 %copy-start.1 = (f32[256,128]{1,0:T(8,128)S(1)}, f32[256,128]{1,0:T(8,128)}, u32[]{:S(2)}) copy-start(f32[256,128]{1,0:T(8,128)} %param.11) | copy-start | bytes 393220
Sparse Core Ops, SparseCore 0:
  9.6 30.6 all-gather.2
  43.9 32.9 reduce-scatter.2
  112.6 21.7 reduce-scatter.4
